TPU v7x, 32 devices: a whole 2x2x4 slice. The times are simulated.
32 devices in a mesh: rows: 8 (over y, x, core), cols: 4 (over z).
Axes of the slice: x: 2, y: 2, z: 4, core: 2. Of those that a mesh axis runs over, the one named last changes fastest.
Arguments:
- token_ids: int32 [16, 2048], P('rows', 'cols'), may hold values from 0 to 131071, as said below
- lengths: int32 [16], P('rows'), may hold values from 1 to 2048
- table: bfloat16 [131072, 512], P('rows', 'cols'), may hold values from -6 to 6
- attn_gain: float32 [512], replicated, may hold values from 0.1 to 1.9
- w_qkv: bfloat16 [512, 1536], replicated, may hold values from -2 to 2
- w_out: bfloat16 [512, 512], replicated, may hold values from -0.25 to 0.25
- mlp_gain: float32 [512], replicated, may hold values from 0.1 to 1.9
- w_in: bfloat16 [512, 4096], replicated, may hold values from -0.25 to 0.25
- w_down: bfloat16 [2048, 512], replicated, may hold values from -0.125 to 0.125
Outputs:
- layer_out: bfloat16 [16, 2048, 512], P('rows', 'cols')
Inputs may be any that keep to these rules, and one draw needn't show every extreme that they name: `token_ids`: ids lie in 0 to 131071. In each aligned block of 2 histories (4096 positions) at most 1365 ids fall in any one block of 16384 consecutive table rows, and in every such block of histories some block of table rows receives exactly 1365.
All inputs are finite; a program needn't handle non-finite values.
Results may differ from a plain program's by a relative error of at most 0.012.
Values may be sent and summed in bfloat16 or wider, within the bound.
A program may use at most 192 MiB of HBM per device.

v0:
```python
import jax
import jax.numpy as jnp
from jax import lax
from jax.sharding import PartitionSpec as P

D = 512
HEADS = 8
FF = 2048


def rms_norm(values_f32, gain):
    mean_sq = jnp.mean(values_f32 * values_f32, axis=-1, keepdims=True)
    return values_f32 * lax.rsqrt(mean_sq + 1e-06) * gain


def local(token_ids, lengths, table, attn_gain, w_qkv, w_out, mlp_gain, w_in, w_down):
    batch_dev, quarter = token_ids.shape
    col_count = lax.axis_size("cols")
    row_count = lax.axis_size("rows")
    full_len = quarter * col_count
    block_rows, col_width = table.shape
    zero_bf = jnp.zeros((), jnp.bfloat16)
    own_ids = lax.all_gather(token_ids, "cols", axis=1, tiled=True)
    flat_ids = own_ids.reshape(-1)
    token_count = flat_ids.shape[0]
    capacity = 8 * token_count // (3 * row_count)
    owner_block = flat_ids // block_rows
    onehot = (owner_block[:, None] == jnp.arange(row_count, dtype=jnp.int32)[None, :]).astype(
        jnp.int32
    )
    slot_rank = jnp.sum((jnp.cumsum(onehot, axis=0) - 1) * onehot, axis=1)
    slot_index = owner_block * capacity + slot_rank
    requests = jnp.full((row_count * capacity,), -1, jnp.int32)
    requests = (
        requests.at[slot_index]
        .set(flat_ids - owner_block * block_rows)
        .reshape(row_count, capacity)
    )
    asked = lax.all_to_all(requests, "rows", split_axis=0, concat_axis=0, tiled=True)
    looked = jnp.take(table, jnp.maximum(asked, 0), axis=0)
    looked = jnp.where((asked >= 0)[..., None], looked, zero_bf)
    returned = lax.all_to_all(looked, "rows", split_axis=0, concat_axis=0, tiled=True)
    embedded = returned.reshape(row_count * capacity, col_width)[slot_index]
    embedded = embedded.reshape(batch_dev, full_len, col_width)
    sequence = lax.all_to_all(embedded, "cols", split_axis=1, concat_axis=2, tiled=True)
    residual = sequence.astype(jnp.float32)
    normed = rms_norm(residual, attn_gain).astype(jnp.bfloat16)
    projected = jnp.einsum("bqe,ef->bqf", normed, w_qkv, preferred_element_type=jnp.float32).astype(
        jnp.bfloat16
    )
    head_dim = D // HEADS
    queries = projected[..., :D].reshape(batch_dev, quarter, HEADS, head_dim)
    keys = projected[..., D : 2 * D]
    values = projected[..., 2 * D :]
    query_pos = lax.axis_index("cols") * quarter + jnp.arange(quarter, dtype=jnp.int32)
    running_max = jnp.full((batch_dev, HEADS, quarter), -1e30, jnp.float32)
    key_piece = lax.all_gather(keys, "cols", axis=1, tiled=True)
    value_piece = lax.all_gather(values, "cols", axis=1, tiled=True)
    piece_len = key_piece.shape[1]
    key_heads = key_piece.reshape(batch_dev, piece_len, HEADS, head_dim)
    value_heads = value_piece.reshape(batch_dev, piece_len, HEADS, head_dim)
    scores = (
        jnp.einsum("bqhd,bkhd->bhqk", queries, key_heads, preferred_element_type=jnp.float32)
        * 0.125
    )
    key_pos = jnp.arange(piece_len, dtype=jnp.int32)
    causal = key_pos[None, :] <= query_pos[:, None]
    inside = key_pos[None, :] < lengths[:, None]
    valid = causal[None, None, :, :] & inside[:, None, None, :]
    scores = jnp.where(valid, scores, -1e30)
    new_max = jnp.maximum(running_max, jnp.max(scores, axis=-1))
    probs = jnp.where(valid, jnp.exp(scores - new_max[..., None]), 0.0)
    running_sum = jnp.sum(probs, axis=-1)
    weighted = jnp.einsum(
        "bhqk,bkhd->bhqd",
        probs.astype(jnp.bfloat16),
        value_heads,
        preferred_element_type=jnp.float32,
    )
    final_max, final_sum, weighted = (new_max, running_sum, weighted)
    summed = weighted / final_sum[..., None]
    attended = (
        jnp.transpose(summed, (0, 2, 1, 3)).reshape(batch_dev, quarter, D).astype(jnp.bfloat16)
    )
    hidden = (
        residual + jnp.einsum("bqe,ef->bqf", attended, w_out, preferred_element_type=jnp.float32)
    ).astype(jnp.bfloat16)
    hidden_f32 = hidden.astype(jnp.float32)
    normed_two = rms_norm(hidden_f32, mlp_gain).astype(jnp.bfloat16)
    gate_up = jnp.einsum("bqe,ef->bqf", normed_two, w_in, preferred_element_type=jnp.float32)
    act = (jax.nn.silu(gate_up[..., :FF]) * gate_up[..., FF:]).astype(jnp.bfloat16)
    return (
        hidden_f32 + jnp.einsum("bqf,fe->bqe", act, w_down, preferred_element_type=jnp.float32)
    ).astype(jnp.bfloat16)


def solution(mesh):
    in_specs = (P("rows", "cols"), P("rows"), P("rows", "cols"), P(), P(), P(), P(), P(), P())
    out_specs = P("rows", "cols", None)
    return jax.shard_map(local, mesh=mesh, in_specs=in_specs, out_specs=out_specs, check_vma=False)
```

profile of v0, /device:TPU:0, one launch (start us, length us, event | category | flops | bytes accessed | tf_op | source)
XLA Modules:
  0.0 414.5 jit_solution(13161058633130101524)
XLA Ops:
  6.5 15.2 %all_gather.9 = s32[2,2048]{1,0:T(2,128)S(1)} all-gather(s32[2,512]{1,0:T(2,128)} %param.9), channel_id=1, replica_groups=mesh['rows'=8,'cols'=4] {'cols'}, dimensions={1}, use_global_device_ids=true | all-gather | bytes 20480 | tf_op jit(solution)/shard_map/all_gather | solution.py:23
  21.8 2.3 reduce-window.6
  25.0 15.5 %scatter_custom_fusion = s32[10920]{0:T(1024)S(1)} fusion(s32[4096]{0:T(1024)S(1)} %bitcast.81, s32[4096]{0:T(1024)S(1)} %get-tuple-element.10, s32[]{:T(128)} %constant.27.clone.1), kind=kCustom, calls=%fused_computation.65 | custom fusion | bytes 43684 | tf_op jit(solution)/shard_map/scatter | solution.py:36
  40.6 8.4 %all_to_all.23 = s32[8,1,1365]{2,1,0:T(1,128)S(1)} all-to-all(s32[8,1,1365]{2,1,0:T(1,128)S(1)} %all_to_all.16), channel_id=1, replica_groups=mesh['rows'=8,'cols'=4] {'rows'}, dimensions={0} | all-to-all | bytes 87360 | tf_op jit(solution)/shard_map/all_to_all | solution.py:39
  49.2 23.7 %gather_fusion = bf16[10920,128]{1,0:T(8,128)(2,1)} fusion(bf16[16384,128]{1,0:T(8,128)(2,1)} %param.11, s32[11264]{0:T(1024)S(1)} %pad_clamp_fusion), kind=kCustom, calls=%fused_computation | custom fusion | bytes 5634720 | tf_op jit(solution)/shard_map/jit(_take)/gather | solution.py:40
  72.9 4.2 %reshape.264 = bf16[8,1365,128]{2,1,0:T(8,128)(2,1)} reshape(bf16[10920,128]{1,0:T(8,128)(2,1)} %gather_fusion) | data formatting | bytes 5591040 | tf_op jit(solution)/shard_map/jit(_take)/gather | solution.py:40
  77.1 10.2 %select_select_fusion = bf16[8,1365,128]{2,1,0:T(8,128)(2,1)} fusion(bf16[8,1365,128]{2,1,0:T(8,128)(2,1)} %reshape.264, pred[8,1365]{1,0:T(8,128)(4,1)S(1)} %get-tuple-element.9, pred[8,1365]{1,0:T(8,128)(4,1)S(1)} %get-tuple-element.8), kind=kLoop, calls=%fused_computation.21 | loop fusion | flops 2795520 | bytes 5612880 | tf_op jit(solution)/shard_map/jit(_where)/select_n | solution.py:41
  87.3 4.4 %all-to-all-start.1 = ((bf16[8,1365,128]{2,1,0:T(8,128)(2,1)}), bf16[8,1365,128]{2,1,0:T(8,128)(2,1)}, u32[]{:S(2)}, u32[]{:S(2)}) async-start(bf16[8,1365,128]{2,1,0:T(8,128)(2,1)} %select_select_fusion), calls=%async_computation.1 | async-start | bytes 5603328 | tf_op jit(solution)/shard_map/all_to_all | solution.py:42
  91.8 34.1 %all-to-all-done.1 = bf16[8,1365,128]{2,1,0:T(8,128)(2,1)} async-done(((bf16[8,1365,128]{2,1,0:T(8,128)(2,1)}), bf16[8,1365,128]{2,1,0:T(8,128)(2,1)}, u32[]{:S(2)}, u32[]{:S(2)}) %all-to-all-start.1) | async-done | bytes 2795552 | tf_op jit(solution)/shard_map/all_to_all | solution.py:42
  125.9 4.2 %reshape.256 = bf16[10920,128]{1,0:T(8,128)(2,1)} reshape(bf16[8,1365,128]{2,1,0:T(8,128)(2,1)} %all-to-all-done.1) | data formatting | bytes 5591040 | tf_op jit(solution)/shard_map/reshape | solution.py:43
  130.1 13.2 %gather_fusion.1 = bf16[4096,128]{1,0:T(8,128)(2,1)S(1)} fusion(bf16[10920,128]{1,0:T(8,128)(2,1)} %reshape.256, s32[4096]{0:T(1024)S(1)} %broadcast_clamp_fusion), kind=kCustom, calls=%fused_computation.1 | custom fusion | bytes 2113536 | tf_op jit(solution)/shard_map/gather | solution.py:43
  143.3 8.7 %copy.57 = bf16[2,2048,128]{2,0,1:T(2,128)(2,1)S(1)} copy(bf16[2,2048,128]{2,1,0:T(8,128)(2,1)S(1)} %bitcast.75) | data formatting | bytes 2097152 | tf_op jit(solution)/shard_map/reshape | solution.py:44
  152.0 27.2 %all_to_all.24 = bf16[2,2048,128]{2,0,1:T(2,128)(2,1)S(1)} all-to-all(bf16[2,2048,128]{2,0,1:T(2,128)(2,1)S(1)} %copy.57), channel_id=1, replica_groups=mesh['rows'=8,'cols'=4] {'cols'}, dimensions={1} | all-to-all | bytes 2097152 | tf_op jit(solution)/shard_map/all_to_all | solution.py:45
  179.2 1.5 copy_convert_fusion
  180.7 2.9 copy.59
  184.3 1.8 fusion.18
  186.2 3.2 convolution_convert_fusion
  189.4 1.7 fusion.44
  191.3 0.7 iota_compare_fusion
  191.9 2.6 broadcast_and_fusion
  194.6 1.3 copy.61
  195.9 76.4 %all-gather.3.cloned.1.call-done = bf16[2,2048,512]{2,1,0:T(8,128)(2,1)} async-done(((bf16[2,512,512]{2,1,0:T(8,128)(2,1)}), bf16[2,2048,512]{2,1,0:T(8,128)(2,1)}) %all-gather.3.cloned.1.call-update) | async-done | bytes 4194320 | tf_op jit(solution)/shard_map/all_gather | solution.py:57
  272.4 6.3 %copy.62 = bf16[2,2048,512]{1,2,0:T(8,128)(2,1)} copy(bf16[2,2048,512]{2,1,0:T(8,128)(2,1)} %all-gather.3.cloned.1.call-done) | data formatting | bytes 8388608 | tf_op jit(solution)/shard_map/all_gather | solution.py:57
  278.6 27.7 %fusion = (f32[2,8,512]{2,1,0:T(8,128)S(1)}, f32[2,8,512,2048]{3,2,1,0:T(8,128)}) fusion(pred[2,512,2048]{2,1,0:T(8,128)(4,1)} %broadcast_and_fusion, bf16[2,512,8,64]{1,3,2,0:T(8,128)(2,1)} %bitcast.74, bf16[2,2048,8,64]{1,3,2,0:T(8,128)(2,1)} %bitcast.72), kind=kOutput, calls=%fused_computation.5 | convolution fusion | flops 2197807104 | bytes 74481664 | tf_op jit(solution)/shard_map/bqhd,bkhd->bhqk/dot_general | solution.py:63
  306.3 22.4 %fusion.1 = f32[2,8,512]{2,1,0:T(8,128)S(1)} fusion(f32[2,8,512,2048]{3,2,1,0:T(8,128)} %get-tuple-element.13, f32[2,8,512]{2,1,0:T(8,128)S(1)} %broadcast_maximum_fusion, pred[2,512,2048]{2,1,0:T(8,128)(4,1)S(1)} %copy-done.1), kind=kLoop, calls=%fused_computation.6 | loop fusion | flops 83877888 | bytes 69271552 | tf_op jit(solution)/shard_map/reduce_sum | solution.py:73
  328.7 24.5 %all-gather.5.cloned.1.call-done = bf16[2,2048,512]{2,1,0:T(8,128)(2,1)} async-done(((bf16[2,512,512]{2,1,0:T(8,128)(2,1)}), bf16[2,2048,512]{2,1,0:T(8,128)(2,1)}) %all-gather.5.cloned.1.call-update) | async-done | bytes 4194320 | tf_op jit(solution)/shard_map/all_gather | solution.py:58
  353.2 6.3 %copy.63 = bf16[2,2048,512]{1,2,0:T(8,128)(2,1)} copy(bf16[2,2048,512]{2,1,0:T(8,128)(2,1)} %all-gather.5.cloned.1.call-done) | data formatting | bytes 8388608 | tf_op jit(solution)/shard_map/all_gather | solution.py:58
  359.5 27.0 %fusion.16 = bf16[2,512,8,64]{1,3,2,0:T(8,128)(2,1)S(1)} fusion(bf16[2,2048,8,64]{1,3,2,0:T(8,128)(2,1)} %bitcast.76, f32[2,8,512,2048]{3,2,1,0:T(8,128)} %get-tuple-element.13, f32[2,8,512]{2,1,0:T(8,128)S(1)} %broadcast_maximum_fusion, pred[2,512,2048]{2,1,0:T(8,128)(4,1)} %broadcast_and_fusion, f32[2,512,8]{1,2,0:T(8,128)S(1)} %bitcast.85), kind=kOutput, calls=%fused_computation.28 | convolution fusion | flops 2232418304 | bytes 74514432 | tf_op jit(solution)/shard_map/bhqk,bkhd->bhqd/dot_general | solution.py:74
  386.5 2.7 fusion.11
  389.4 8.3 %fusion.7 = f32[2,512,4096]{2,1,0:T(8,128)} fusion(bf16[512,4096]{1,0:T(8,128)(2,1)S(1)} %copy-done.4, bf16[2,512,512]{1,2,0:T(8,128)(2,1)S(1)} %get-tuple-element.15, f32[512]{0:T(512)S(1)} %copy-done.5, f32[2,512]{1,0:T(2,128)S(1)} %add_rsqrt_fusion), kind=kOutput, calls=%fused_computation.12 | convolution fusion | flops 4297064448 | bytes 22026240 | tf_op jit(solution)/shard_map/bqe,ef->bqf/dot_general | solution.py:90
  397.8 8.6 %fusion.14 = bf16[2,512,512]{1,2,0:T(8,128)(2,1)S(1)} fusion(bf16[2,512,512]{1,2,0:T(8,128)(2,1)S(1)} %get-tuple-element.15, bf16[2048,512]{1,0:T(8,128)(2,1)S(1)} %copy-done, f32[2,512,4096]{2,1,0:T(8,128)} %fusion.7), kind=kOutput, calls=%fused_computation.25 | convolution fusion | flops 2161639424 | bytes 20971520 | tf_op jit(solution)/shard_map/bqf,fe->bqe/dot_general | solution.py:93
  406.3 1.3 copy.68
  (41 shorter events, 2.3 us)
Async XLA Ops:
  6.5 391.2 %copy-start = (bf16[2048,512]{1,0:T(8,128)(2,1)S(1)}, bf16[2048,512]{1,0:T(8,128)(2,1)}, u32[]{:S(2)}) copy-start(bf16[2048,512]{1,0:T(8,128)(2,1)} %param.17) | copy-start | bytes 6291460
  87.3 38.6 %all-to-all-start.1 = ((bf16[8,1365,128]{2,1,0:T(8,128)(2,1)}), bf16[8,1365,128]{2,1,0:T(8,128)(2,1)}, u32[]{:S(2)}, u32[]{:S(2)}) async-start(bf16[8,1365,128]{2,1,0:T(8,128)(2,1)} %select_select_fusion), calls=%async_computation.1 | async-start | bytes 5603328 | tf_op jit(solution)/shard_map/all_to_all | solution.py:42
  91.7 180.7 %all-gather.3.cloned.1.call-start = ((), (), s32[]{:S(2)}) async-start(), calls=%async_computation.3 | async-start | bytes 5242880 | tf_op jit(solution)/shard_map/all_gather | solution.py:57
  179.2 5.1 %copy-start.2 = (f32[512]{0:T(512)S(1)}, f32[512]{0:T(512)}, u32[]{:S(2)}) copy-start(f32[512]{0:T(512)} %param.12) | copy-start | bytes 6148
  189.4 1.8 copy-start.3
  191.1 162.1 %all-gather.5.cloned.1.call-start = ((), (), s32[]{:S(2)}) async-start(), calls=%async_computation.4 | async-start | bytes 5242880 | tf_op jit(solution)/shard_map/all_gather | solution.py:58
  278.6 27.7 %copy-start.1 = (pred[2,512,2048]{2,1,0:T(8,128)(4,1)S(1)}, pred[2,512,2048]{2,1,0:T(8,128)(4,1)}, u32[]{:S(2)}) copy-start(pred[2,512,2048]{2,1,0:T(8,128)(4,1)} %broadcast_and_fusion) | copy-start | bytes 6291460
  386.5 3.0 copy-start.4
  386.5 3.0 copy-start.5
Sparse Core Ops, SparseCore 0:
  191.2 81.0 all-gather.2
  273.9 79.2 all-gather.4
where the time goes:
time: 415 us
  waiting for transfers between devices  135 us (33%)
  local copies, waits for them, and re-layouts  90.2 us (22%)
  matrix products  77.4 us (19%)
  blocking collectives  50.8 us (12%)
  other arithmetic  42.8 us (10%)
  between operations  13.7 us (3%)
  starting transfers between devices  4.49 us (1%)
    all_gather x1, waiting for transfers between devices, local(): key_piece = lax.all_gather(keys, 'cols', axis=1, tiled=True)  76.4 us
    all_to_all x1, waiting for transfers between devices, local(): lax.all_to_all(looked, 'rows', split_axis=0, concat_axis=0, tiled=True)  34.1 us
    gather x2, local copies, waits for them, and re-layouts, local(): looked = jnp.take(table, jnp.maximum(asked, 0), axis=0)  27.9 us
    dot_general x1, matrix products, local(): jnp.einsum('bqhd,bkhd->bhqk', queries, key_heads, preferred_element_type=...  27.7 us
    all_to_all x1, blocking collectives, local(): lax.all_to_all(embedded, 'cols', split_axis=1, concat_axis=2, tiled=True)  27.2 us
    dot_general x1, matrix products, local(): jnp.einsum('bhqk,bkhd->bhqd', probs.astype(jnp.bfloat16), value_heads, pr...  27 us
    all_gather x1, waiting for transfers between devices, local(): value_piece = lax.all_gather(values, 'cols', axis=1, tiled=True)  24.5 us
    reduce_sum x1, other arithmetic, local(): running_sum = jnp.sum(probs, axis=-1)  22.4 us
  transfers between devices with their start and end apart: 3, of which 3 were waited for; matrix products, arithmetic and copies ran while one was open for 15% of the time, Pallas kernels for 0%

commit v1 on v0

--- a/solution.py
+++ b/solution.py
@@ -55,7 +55,16 @@
     query_pos = lax.axis_index("cols") * quarter + jnp.arange(quarter, dtype=jnp.int32)
     running_max = jnp.full((batch_dev, HEADS, quarter), -1e30, jnp.float32)
     key_piece = lax.all_gather(keys, "cols", axis=1, tiled=True)
-    value_piece = lax.all_gather(values, "cols", axis=1, tiled=True)
+    ways = lax.axis_size("cols")
+    up = [(d, (d + 1) % ways) for d in range(ways)]
+    down = [(d, (d - 1) % ways) for d in range(ways)]
+    earlier, later = ([values], [values])
+    for _ in range(ways // 2):
+        earlier.append(lax.ppermute(earlier[-1], "cols", up))
+    for _ in range((ways - 1) // 2):
+        later.append(lax.ppermute(later[-1], "cols", down))
+    line = jnp.concatenate([*earlier[::-1], *later[1:]], axis=1)
+    value_piece = jnp.roll(line, (lax.axis_index("cols") - ways // 2) * values.shape[1], axis=1)
     piece_len = key_piece.shape[1]
     key_heads = key_piece.reshape(batch_dev, piece_len, HEADS, head_dim)
     value_heads = value_piece.reshape(batch_dev, piece_len, HEADS, head_dim)

time: 415 us -> 460 us (1.11)
  waiting for transfers between devices: 135 us -> 166 us
  local copies, waits for them, and re-layouts: 90.2 us -> 100 us
    ppermute x0 -> x3, waiting for transfers between devices: none -> 65.4 us  [the longest x2 48.6 us: local(): earlier.append(lax.ppermute(earlier[-1], 'cols', up))]
    all_gather x1 -> x0, waiting for transfers between devices: 24.5 us -> none  [local(): value_piece = lax.all_gather(values, 'cols', axis=1, tiled=True)]
    dynamic_slice x0 -> x2, local copies, waits for them, and re-layouts: none -> 10.9 us  [local(): jnp.roll(line, (lax.axis_index('cols') - ways // 2) * values.shape[1], ax...]
    all_gather x1, waiting for transfers between devices: 76.4 us -> 66.6 us  [local(): key_piece = lax.all_gather(keys, 'cols', axis=1, tiled=True)]
    all_gather x1 -> x0, local copies, waits for them, and re-layouts: 6.28 us -> none  [local(): value_piece = lax.all_gather(values, 'cols', axis=1, tiled=True)]
  transfers between devices with their start and end apart: 3 -> 5, of which waited for: 3 -> 5; matrix products, arithmetic and copies ran while one was open for 15% -> 4% of each run, Pallas kernels for 0% -> 0%
where the time goes in v1:
time: 460 us; the launch traced here: 459 us
  waiting for transfers between devices  166 us (36%)
  local copies, waits for them, and re-layouts  100 us (22%)
  matrix products  76.8 us (17%)
  blocking collectives  50.8 us (11%)
  other arithmetic  42.8 us (9%)
  between operations  13.7 us (3%)
  starting transfers between devices  8.54 us (2%)
    all_gather x1, waiting for transfers between devices, local(): key_piece = lax.all_gather(keys, 'cols', axis=1, tiled=True)  66.6 us
    ppermute x2, waiting for transfers between devices, local(): earlier.append(lax.ppermute(earlier[-1], 'cols', up))  48.6 us
    all_to_all x1, waiting for transfers between devices, local(): lax.all_to_all(looked, 'rows', split_axis=0, concat_axis=0, tiled=True)  34.1 us
    gather x2, local copies, waits for them, and re-layouts, local(): looked = jnp.take(table, jnp.maximum(asked, 0), axis=0)  27.9 us
    all_to_all x1, blocking collectives, local(): lax.all_to_all(embedded, 'cols', split_axis=1, concat_axis=2, tiled=True)  27.2 us
    dot_general x1, matrix products, local(): jnp.einsum('bqhd,bkhd->bhqk', queries, key_heads, preferred_element_type=...  27.1 us
    dot_general x1, matrix products, local(): jnp.einsum('bhqk,bkhd->bhqd', probs.astype(jnp.bfloat16), value_heads, pr...  26.9 us
    reduce_sum x1, other arithmetic, local(): running_sum = jnp.sum(probs, axis=-1)  22.4 us
  transfers between devices with their start and end apart: 5, of which 5 were waited for; matrix products, arithmetic and copies ran while one was open for 4% of the time, Pallas kernels for 0%

profile of v1, /device:TPU:0, one launch (start us, length us, event | category | flops | bytes accessed | tf_op | source)
XLA Modules:
  0.0 459.3 jit_solution(13227516693580612674)
XLA Ops:
  6.5 15.2 %all_gather.6 = s32[2,2048]{1,0:T(2,128)S(1)} all-gather(s32[2,512]{1,0:T(2,128)} %param.9), channel_id=1, replica_groups=mesh['rows'=8,'cols'=4] {'cols'}, dimensions={1}, use_global_device_ids=true | all-gather | bytes 20480 | tf_op jit(solution)/shard_map/all_gather | solution.py:23
  21.8 2.3 reduce-window.6
  25.0 15.5 %scatter_custom_fusion = s32[10920]{0:T(1024)S(1)} fusion(s32[4096]{0:T(1024)S(1)} %bitcast.82, s32[4096]{0:T(1024)S(1)} %get-tuple-element.10, s32[]{:T(128)} %constant.74.clone.1), kind=kCustom, calls=%fused_computation.65 | custom fusion | bytes 43684 | tf_op jit(solution)/shard_map/scatter | solution.py:36
  40.6 8.4 %all_to_all.23 = s32[8,1,1365]{2,1,0:T(1,128)S(1)} all-to-all(s32[8,1,1365]{2,1,0:T(1,128)S(1)} %all_to_all.16), channel_id=1, replica_groups=mesh['rows'=8,'cols'=4] {'rows'}, dimensions={0} | all-to-all | bytes 87360 | tf_op jit(solution)/shard_map/all_to_all | solution.py:39
  49.2 23.7 %gather_fusion = bf16[10920,128]{1,0:T(8,128)(2,1)} fusion(bf16[16384,128]{1,0:T(8,128)(2,1)} %param.11, s32[11264]{0:T(1024)S(1)} %pad_clamp_fusion), kind=kCustom, calls=%fused_computation | custom fusion | bytes 5634720 | tf_op jit(solution)/shard_map/jit(_take)/gather | solution.py:40
  72.9 4.2 reshape.264
  77.1 10.2 %select_select_fusion = bf16[8,1365,128]{2,1,0:T(8,128)(2,1)} fusion(bf16[8,1365,128]{2,1,0:T(8,128)(2,1)} %reshape.264, pred[8,1365]{1,0:T(8,128)(4,1)S(1)} %get-tuple-element.9, pred[8,1365]{1,0:T(8,128)(4,1)S(1)} %get-tuple-element.8), kind=kLoop, calls=%fused_computation.21 | loop fusion | flops 2795520 | bytes 5612880 | tf_op jit(solution)/shard_map/jit(_where)/select_n | solution.py:41
  87.3 4.4 all-to-all-start.1
  91.8 34.1 %all-to-all-done.1 = bf16[8,1365,128]{2,1,0:T(8,128)(2,1)} async-done(((bf16[8,1365,128]{2,1,0:T(8,128)(2,1)}), bf16[8,1365,128]{2,1,0:T(8,128)(2,1)}, u32[]{:S(2)}, u32[]{:S(2)}) %all-to-all-start.1) | async-done | bytes 2795552 | tf_op jit(solution)/shard_map/all_to_all | solution.py:42
  125.9 4.2 reshape.256
  130.1 13.2 %gather_fusion.1 = bf16[4096,128]{1,0:T(8,128)(2,1)S(1)} fusion(bf16[10920,128]{1,0:T(8,128)(2,1)} %reshape.256, s32[4096]{0:T(1024)S(1)} %broadcast_clamp_fusion), kind=kCustom, calls=%fused_computation.1 | custom fusion | bytes 2113536 | tf_op jit(solution)/shard_map/gather | solution.py:43
  143.3 8.7 %copy.56 = bf16[2,2048,128]{2,0,1:T(2,128)(2,1)S(1)} copy(bf16[2,2048,128]{2,1,0:T(8,128)(2,1)S(1)} %bitcast.76) | data formatting | bytes 2097152 | tf_op jit(solution)/shard_map/reshape | solution.py:44
  152.0 27.2 %all_to_all.24 = bf16[2,2048,128]{2,0,1:T(2,128)(2,1)S(1)} all-to-all(bf16[2,2048,128]{2,0,1:T(2,128)(2,1)S(1)} %copy.56), channel_id=1, replica_groups=mesh['rows'=8,'cols'=4] {'cols'}, dimensions={1} | all-to-all | bytes 2097152 | tf_op jit(solution)/shard_map/all_to_all | solution.py:45
  181.4 2.9 copy.58
  186.2 3.2 convolution_convert_fusion
  189.8 24.6 %collective-permute-done = bf16[2,512,512]{2,1,0:T(8,128)(2,1)S(1)} collective-permute-done((bf16[2,512,512]{2,1,0:T(8,128)(2,1)S(1)}, bf16[2,512,512]{2,1,0:T(8,128)(2,1)S(1)}, u32[]{:S(2)}, u32[]{:S(2)}) %collective-permute-start) | collective-permute-done | bytes 1048608 | tf_op jit(solution)/shard_map/ppermute | solution.py:63
  214.4 3.8 collective-permute-start.2
  218.2 24.0 %collective-permute-done.1 = bf16[2,512,512]{2,1,0:T(8,128)(2,1)S(1)} collective-permute-done((bf16[2,512,512]{2,1,0:T(8,128)(2,1)S(1)}, bf16[2,512,512]{2,1,0:T(8,128)(2,1)S(1)}, u32[]{:S(2)}, u32[]{:S(2)}) %collective-permute-start.1) | collective-permute-done | bytes 1048608 | tf_op jit(solution)/shard_map/ppermute | solution.py:63
  242.4 16.8 %collective-permute-done.2 = bf16[2,512,512]{2,1,0:T(8,128)(2,1)S(1)} collective-permute-done((bf16[2,512,512]{2,1,0:T(8,128)(2,1)S(1)}, bf16[2,512,512]{2,1,0:T(8,128)(2,1)S(1)}, u32[]{:S(2)}, u32[]{:S(2)}) %collective-permute-start.2) | collective-permute-done | bytes 1048608 | tf_op jit(solution)/shard_map/ppermute | solution.py:65
  261.1 3.2 copy-done.2
  265.1 2.6 broadcast_and_fusion
  267.8 2.4 copy.60
  271.2 4.4 constant_dynamic-slice_fusion
  275.6 6.5 %copy.62 = bf16[2,2048,512]{1,2,0:T(8,128)(2,1)} copy(bf16[2,2048,512]{2,1,0:T(8,128)(2,1)} %constant_dynamic-slice_fusion) | data formatting | bytes 8388608 | tf_op jit(solution)/shard_map/jit(_roll_dynamic)/dynamic_slice | solution.py:67
  282.0 66.6 %all-gather.2.cloned.1.call-done = bf16[2,2048,512]{2,1,0:T(8,128)(2,1)} async-done(((bf16[2,512,512]{2,1,0:T(8,128)(2,1)}), bf16[2,2048,512]{2,1,0:T(8,128)(2,1)}) %all-gather.2.cloned.1.call-update) | async-done | bytes 4194320 | tf_op jit(solution)/shard_map/all_gather | solution.py:57
  348.6 6.3 %copy.61 = bf16[2,2048,512]{1,2,0:T(8,128)(2,1)} copy(bf16[2,2048,512]{2,1,0:T(8,128)(2,1)} %all-gather.2.cloned.1.call-done) | data formatting | bytes 8388608 | tf_op jit(solution)/shard_map/all_gather | solution.py:57
  354.9 27.1 %fusion = (f32[2,8,512]{2,1,0:T(8,128)S(1)}, f32[2,8,512,2048]{3,2,1,0:T(8,128)}) fusion(pred[2,512,2048]{2,1,0:T(8,128)(4,1)} %broadcast_and_fusion, bf16[2,512,8,64]{1,3,2,0:T(8,128)(2,1)} %bitcast.75, bf16[2,2048,8,64]{1,3,2,0:T(8,128)(2,1)} %bitcast.73), kind=kOutput, calls=%fused_computation.5 | convolution fusion | flops 2197807104 | bytes 74481664 | tf_op jit(solution)/shard_map/bqhd,bkhd->bhqk/dot_general | solution.py:72
  382.0 22.4 %fusion.1 = f32[2,8,512]{2,1,0:T(8,128)S(1)} fusion(f32[2,8,512,2048]{3,2,1,0:T(8,128)} %get-tuple-element.13, f32[2,8,512]{2,1,0:T(8,128)S(1)} %broadcast_maximum_fusion, pred[2,512,2048]{2,1,0:T(8,128)(4,1)S(1)} %copy-done.1), kind=kLoop, calls=%fused_computation.6 | loop fusion | flops 83877888 | bytes 69271552 | tf_op jit(solution)/shard_map/reduce_sum | solution.py:82
  404.3 26.9 %fusion.16 = bf16[2,512,8,64]{1,3,2,0:T(8,128)(2,1)S(1)} fusion(bf16[2,2048,8,64]{1,3,2,0:T(8,128)(2,1)} %bitcast.77, f32[2,8,512,2048]{3,2,1,0:T(8,128)} %get-tuple-element.13, f32[2,8,512]{2,1,0:T(8,128)S(1)} %broadcast_maximum_fusion, pred[2,512,2048]{2,1,0:T(8,128)(4,1)} %broadcast_and_fusion, f32[2,512,8]{1,2,0:T(8,128)S(1)} %bitcast.86), kind=kOutput, calls=%fused_computation.28 | convolution fusion | flops 2232418304 | bytes 74514432 | tf_op jit(solution)/shard_map/bhqk,bkhd->bhqd/dot_general | solution.py:83
  431.3 2.7 fusion.11
  434.2 8.3 %fusion.7 = f32[2,512,4096]{2,1,0:T(8,128)} fusion(bf16[512,4096]{1,0:T(8,128)(2,1)S(1)} %copy-done.5, bf16[2,512,512]{1,2,0:T(8,128)(2,1)S(1)} %get-tuple-element.15, f32[512]{0:T(512)S(1)} %copy-done.6, f32[2,512]{1,0:T(2,128)S(1)} %add_rsqrt_fusion), kind=kOutput, calls=%fused_computation.12 | convolution fusion | flops 4297064448 | bytes 22026240 | tf_op jit(solution)/shard_map/bqe,ef->bqf/dot_general | solution.py:99
  442.6 8.6 %fusion.14 = bf16[2,512,512]{1,2,0:T(8,128)(2,1)S(1)} fusion(bf16[2,512,512]{1,2,0:T(8,128)(2,1)S(1)} %get-tuple-element.15, bf16[2048,512]{1,0:T(8,128)(2,1)S(1)} %copy-done, f32[2,512,4096]{2,1,0:T(8,128)} %fusion.7), kind=kOutput, calls=%fused_computation.25 | convolution fusion | flops 2161639424 | bytes 20971520 | tf_op jit(solution)/shard_map/bqf,fe->bqe/dot_general | solution.py:102
  (55 shorter events, 11.0 us)
Async XLA Ops:
  6.5 436.0 %copy-start = (bf16[2048,512]{1,0:T(8,128)(2,1)S(1)}, bf16[2048,512]{1,0:T(8,128)(2,1)}, u32[]{:S(2)}) copy-start(bf16[2048,512]{1,0:T(8,128)(2,1)} %param.17) | copy-start | bytes 6291460
  87.3 38.6 %all-to-all-start.1 = ((bf16[8,1365,128]{2,1,0:T(8,128)(2,1)}), bf16[8,1365,128]{2,1,0:T(8,128)(2,1)}, u32[]{:S(2)}, u32[]{:S(2)}) async-start(bf16[8,1365,128]{2,1,0:T(8,128)(2,1)} %select_select_fusion), calls=%async_computation.1 | async-start | bytes 5603328 | tf_op jit(solution)/shard_map/all_to_all | solution.py:42
  91.7 256.9 %all-gather.2.cloned.1.call-start = ((), (), s32[]{:S(2)}) async-start(), calls=%async_computation.3 | async-start | bytes 5242880 | tf_op jit(solution)/shard_map/all_gather | solution.py:57
  179.2 5.1 %copy-start.3 = (f32[512]{0:T(512)S(1)}, f32[512]{0:T(512)}, u32[]{:S(2)}) copy-start(f32[512]{0:T(512)} %param.12) | copy-start | bytes 6148
  189.5 24.9 %collective-permute-start = (bf16[2,512,512]{2,1,0:T(8,128)(2,1)S(1)}, bf16[2,512,512]{2,1,0:T(8,128)(2,1)S(1)}, u32[]{:S(2)}, u32[]{:S(2)}) collective-permute-start(bf16[2,512,512]{2,1,0:T(8,128)(2,1)S(1)} %slice.35), channel_id=1, source_target_pairs={{0,1},{1,2},{2,3},{3,0},{4,5},{5,6},{6,7},{7,4},{8,9},{9,10},{10,1... | collective-permute-start | bytes 3145736 | tf_op jit(solution)/shard_map/ppermute | solution.py:63
  214.4 27.8 %collective-permute-start.1 = (bf16[2,512,512]{2,1,0:T(8,128)(2,1)S(1)}, bf16[2,512,512]{2,1,0:T(8,128)(2,1)S(1)}, u32[]{:S(2)}, u32[]{:S(2)}) collective-permute-start(bf16[2,512,512]{2,1,0:T(8,128)(2,1)S(1)} %collective-permute-done), channel_id=1, source_target_pairs={{0,1},{1,2},{2,3},{3,0},{4,5},{5,6},{6,7},{7,4},{8,9},{9,10},{10,1... | collective-permute-start | bytes 3145736 | tf_op jit(solution)/shard_map/ppermute | solution.py:63
  214.4 44.9 %collective-permute-start.2 = (bf16[2,512,512]{2,1,0:T(8,128)(2,1)S(1)}, bf16[2,512,512]{2,1,0:T(8,128)(2,1)S(1)}, u32[]{:S(2)}, u32[]{:S(2)}) collective-permute-start(bf16[2,512,512]{2,1,0:T(8,128)(2,1)S(1)} %slice.35), channel_id=1, source_target_pairs={{0,3},{1,0},{2,1},{3,2},{4,7},{5,4},{6,5},{7,6},{8,11},{9,8},{10,9... | collective-permute-start | bytes 3145736 | tf_op jit(solution)/shard_map/ppermute | solution.py:65
  259.5 4.9 %copy-start.4 = (s32[2]{0:T(128)S(1)}, s32[2]{0:T(128)}, u32[]{:S(2)}) copy-start(s32[2]{0:T(128)} %param.10) | copy-start | bytes 28
  261.1 3.2 copy-start.2
  354.9 27.1 %copy-start.1 = (pred[2,512,2048]{2,1,0:T(8,128)(4,1)S(1)}, pred[2,512,2048]{2,1,0:T(8,128)(4,1)}, u32[]{:S(2)}) copy-start(pred[2,512,2048]{2,1,0:T(8,128)(4,1)} %broadcast_and_fusion) | copy-start | bytes 6291460
  431.2 3.0 copy-start.5
  431.3 3.0 copy-start.6
Sparse Core Ops, SparseCore 0:
  264.5 84.0 all-gather.1
